TPU v7x, 16 devices: a 4x2x1 block of a 4x4x4 slice. The times are simulated.
16 devices in a mesh: dp: 4 (over y, z, core), tp: 4 (over x).
Axes of the slice: x: 4, y: 2, z: 1, core: 2. Of those that a mesh axis runs over, the one named last changes fastest.
The devices are a block of a 4x4x4 slice.
Arguments:
- x: bfloat16 [256, 4096], P('dp'), parts along dimension 0
- k_cache: bfloat16 [256, 1024, 64, 64], P('dp', None, 'tp'), parts along dimension 0
- v_cache: bfloat16 [256, 1024, 64, 64], P('dp', None, 'tp'), parts along dimension 0
- gain_a: bfloat16 [4096], replicated
- wq: bfloat16 [4096, 4096], P(None, 'tp')
- wo: bfloat16 [4096, 4096], P('tp')
- gain_m: bfloat16 [4096], replicated
- w_gate: bfloat16 [4096, 10240], P(None, 'tp')
- w_up: bfloat16 [4096, 10240], P(None, 'tp')
- w_down: bfloat16 [10240, 4096], P('tp')
Outputs:
- output: bfloat16 [256, 4096], P('dp'), parts along dimension 0
There are 4 independent parts. A program takes and returns all parts, laid end to end along the dimension named above; an argument that names none is the same for every part.
All inputs are finite; a program needn't handle non-finite values.
Results may differ from a plain program's by a relative error of at most 0.017.
Values are sent between devices in bfloat16 or wider.
A program may use at most 1.5 GiB of HBM per device.

v0:
```python
import jax
import jax.numpy as jnp
from jax import lax
from jax.sharding import PartitionSpec as P

HEAD = 64
THETA = 10000


def normed(x, gain):
    wide = x.astype(jnp.float32)
    scale = lax.rsqrt(jnp.mean(wide * wide, -1, keepdims=True) + 1e-6)
    return (wide * scale * gain.astype(jnp.float32)).astype(jnp.bfloat16)


def turned(t, place, theta):
    half = t.shape[-1] // 2
    angle = place.astype(jnp.float32)[:, None] * theta ** (-jnp.arange(half, dtype=jnp.float32) / half)
    cos, sin = jnp.cos(angle)[:, None], jnp.sin(angle)[:, None]
    a, b = t[..., :half].astype(jnp.float32), t[..., half:].astype(jnp.float32)
    return jnp.concatenate([a * cos - b * sin, b * cos + a * sin], -1).astype(jnp.bfloat16)


def matmul(a, w):
    return jnp.dot(a, w, preferred_element_type=jnp.float32).astype(jnp.bfloat16)


def einsum(form, a, b):
    return jnp.einsum(form, a.astype(jnp.float32), b.astype(jnp.float32))


def seen_by(a, wq, k_cache, v_cache, head, theta):
    batch, cache, kv_heads = k_cache.shape[:3]
    place = jnp.full((batch,), cache - 1)
    q = turned(matmul(a, wq).reshape(batch, -1, head), place, theta).reshape(batch, kv_heads, -1, head)
    scores = einsum("bgsd,bugd->bgsu", q, k_cache) * head**-0.5
    weights = jax.nn.softmax(scores, -1).astype(jnp.bfloat16)
    return einsum("bgsu,bugd->bgsd", weights, v_cache).astype(jnp.bfloat16).reshape(batch, -1)


def hidden_of(b, w_gate, w_up):
    gate = jnp.dot(b, w_gate, preferred_element_type=jnp.float32)
    up = jnp.dot(b, w_up, preferred_element_type=jnp.float32)
    return (jax.nn.silu(gate) * up).astype(jnp.bfloat16)


def solution(mesh):
    def added(t, term):
        return (t.astype(jnp.float32) + lax.psum(term.astype(jnp.bfloat16), "tp").astype(jnp.float32)).astype(jnp.bfloat16)

    def step(x, k_cache, v_cache, gain_a, wq, wo, gain_m, w_gate, w_up, w_down):
        seen = seen_by(normed(x, gain_a), wq, k_cache, v_cache, HEAD, THETA)
        h = added(x, jnp.dot(seen, wo, preferred_element_type=jnp.float32))
        return added(h, jnp.dot(hidden_of(normed(h, gain_m), w_gate, w_up), w_down, preferred_element_type=jnp.float32))

    states, cache, columns, rows_of = P("dp", None), P("dp", None, "tp", None), P(None, "tp"), P("tp", None)
    return jax.shard_map(
        step,
        mesh=mesh,
        in_specs=(states, cache, cache, P(None), columns, rows_of, P(None), columns, columns, rows_of),
        out_specs=states,
        check_vma=False,
    )
```

profile of v0, /device:TPU:112, one launch (start us, length us, event | category | flops | bytes accessed | tf_op | source)
XLA Modules:
  0.0 228.2 jit_solution(11192106198663915019)
XLA Ops:
  6.5 0.0 all-reduce.3.cloned.1.call-start
  6.6 0.7 convert_element_type.66
  7.3 1.2 fusion.9
  8.6 5.2 %convolution_convert_fusion.2 = bf16[64,1024]{1,0:T(8,128)(2,1)S(1)} fusion(bf16[4096,1024]{1,0:T(8,128)(2,1)} %param.14, bf16[64,4096]{1,0:T(8,128)(2,1)} %param.10, f32[4096]{0:T(1024)S(1)} %convert_element_type.66, f32[64]{0:T(128)S(1)} %add_rsqrt_fusion.1), kind=kOutput, calls=%fused_computation.20 | convolution fusion | flops 537985024 | bytes 9060608 | tf_op jit(solution)/shard_map/dot_general | solution.py:25
  13.8 0.2 copy.11
  14.0 0.2 fusion.24
  14.1 0.1 maximum_bitcast_fusion
  14.2 0.5 copy.12
  14.7 44.7 %fusion.37 = f32[64,16,1,1024]{3,2,1,0:T(1,128)} fusion(bf16[64,16,64,1]{2,3,1,0:T(2,128)(2,1)S(1)} %copy.12, bf16[64,1024,16,64]{1,3,2,0:T(8,128)(2,1)} %param.11), kind=kOutput, calls=%fused_computation.53 | convolution fusion | flops 134217728 | bytes 138543104 | tf_op jit(solution)/shard_map/bgsd,bugd->bgsu/dot_general | solution.py:29
  59.4 0.0 copy-start
  59.4 3.3 %fusion.1 = f32[64,16,1024]{2,1,0:T(8,128)S(1)} fusion(f32[64,16,1,1024]{3,2,1,0:T(1,128)} %fusion.37), kind=kOutput, calls=%fused_computation.1 | output fusion | flops 1050623 | bytes 8388608 | tf_op jit(solution)/shard_map/sub | solution.py:37
  62.7 0.2 copy-done
  62.9 2.2 fusion.7
  65.1 47.1 %fusion.2 = f32[64,16,1,64]{3,2,1,0:T(1,128)S(1)} fusion(bf16[64,1024,16,64]{1,3,2,0:T(8,128)(2,1)} %param.12, bf16[64,16,1024,1]{2,1,0,3:T(8,128)(2,1)S(1)} %fusion.7), kind=kOutput, calls=%fused_computation.5 | convolution fusion | flops 134217728 | bytes 136577024 | tf_op jit(solution)/shard_map/bgsu,bugd->bgsd/dot_general | solution.py:29
  112.1 0.0 copy-start.2
  112.2 0.0 copy-start.1
  112.2 0.2 reshape.62
  112.4 5.7 %convolution_convert_fusion.1 = bf16[64,4096]{1,0:T(8,128)(2,1)} fusion(bf16[64,1024]{1,0:T(8,128)(2,1)S(1)} %reshape.62, bf16[1024,4096]{1,0:T(8,128)(2,1)} %param.15), kind=kOutput, calls=%fused_computation.3 | convolution fusion | flops 537133056 | bytes 9043968 | tf_op jit(solution)/shard_map/dot_general | solution.py:53
  118.2 0.1 all-reduce.3.cloned.1.call-update
  118.2 0.2 all-reduce.5.cloned.1.call-start
  118.5 0.0 copy-done.2
  118.5 37.4 %all-reduce.3.cloned.1.call-done = bf16[64,4096]{1,0:T(8,128)(2,1)} async-done(((bf16[64,4096]{1,0:T(8,128)(2,1)}), bf16[64,4096]{1,0:T(8,128)(2,1)}) %all-reduce.3.cloned.1.call-update) | async-done | bytes 524304 | tf_op jit(solution)/shard_map/psum | solution.py:49
  155.9 0.0 copy-done.1
  155.9 1.3 fusion.13
  157.2 9.0 %fusion.29 = f32[64,2560]{1,0:T(8,128)S(1)} fusion(bf16[4096,2560]{1,0:T(8,128)(2,1)} %param.17, bf16[64,4096]{1,0:T(8,128)(2,1)S(1)} %get-tuple-element.6, f32[4096]{0:T(1024)S(1)} %convert_element_type.77, f32[64]{0:T(128)S(1)} %add_rsqrt_fusion), kind=kOutput, calls=%fused_computation.44 | convolution fusion | flops 1343225856 | bytes 22167808 | tf_op jit(solution)/shard_map/dot_general | solution.py:42
  166.2 17.8 %convolution_convert_fusion = bf16[64,4096]{1,0:T(8,128)(2,1)} fusion(bf16[2560,4096]{1,0:T(8,128)(2,1)} %param.19, bf16[4096,2560]{1,0:T(8,128)(2,1)} %param.18, f32[64,2560]{1,0:T(8,128)S(1)} %fusion.29, bf16[64,4096]{1,0:T(8,128)(2,1)S(1)} %get-tuple-element.6, f32[4096]{0:T(1024)S(1)} %convert_element_type.77, f32[64]{0:T(128)S(1)} %add_rsqrt_fusion), kind=kOutput, calls=%fused_computation.2 | convolution fusion | flops 2686648320 | bytes 43663616 | tf_op jit(solution)/shard_map/dot_general | solution.py:54
  184.0 0.1 all-reduce.5.cloned.1.call-update
  184.1 35.3 %all-reduce.5.cloned.1.call-done = bf16[64,4096]{1,0:T(8,128)(2,1)} async-done(((bf16[64,4096]{1,0:T(8,128)(2,1)}), bf16[64,4096]{1,0:T(8,128)(2,1)}) %all-reduce.5.cloned.1.call-update) | async-done | bytes 524304 | tf_op jit(solution)/shard_map/psum | solution.py:49
  219.3 2.0 fusion.16
  (5 shorter events, 0.1 us)
Async XLA Ops:
  6.5 149.3 %all-reduce.3.cloned.1.call-start = ((), (), s32[]{:S(2)}) async-start(), calls=%async_computation | async-start | bytes 1048576 | tf_op jit(solution)/shard_map/psum | solution.py:49
  59.4 3.4 %copy-start = (f32[64,16,1,1024]{3,2,1,0:T(1,128)S(1)}, f32[64,16,1,1024]{3,2,1,0:T(1,128)}, u32[]{:S(2)}) copy-start(f32[64,16,1,1024]{3,2,1,0:T(1,128)} %fusion.37) | copy-start | bytes 12582916
  112.1 6.3 %copy-start.2 = (bf16[4096]{0:T(1024)(128)(2,1)S(1)}, bf16[4096]{0:T(1024)(128)(2,1)}, u32[]{:S(2)}) copy-start(bf16[4096]{0:T(1024)(128)(2,1)} %param.16) | copy-start | bytes 24580
  112.2 43.7 %copy-start.1 = (bf16[64,4096]{1,0:T(8,128)(2,1)S(1)}, bf16[64,4096]{1,0:T(8,128)(2,1)}, u32[]{:S(2)}) copy-start(bf16[64,4096]{1,0:T(8,128)(2,1)} %param.10) | copy-start | bytes 1572868
  118.2 101.1 %all-reduce.5.cloned.1.call-start = ((), (), s32[]{:S(2)}) async-start(), calls=%async_computation.1 | async-start | bytes 1048576 | tf_op jit(solution)/shard_map/psum | solution.py:49
Sparse Core Ops, SparseCore 0:
  118.3 37.4 all-reduce.2
  184.2 35.1 all-reduce.4
where the time goes:
time: 229 us; the launch traced here: 228 us
  matrix products  129 us (56%)
  waiting for transfers between devices  72.8 us (32%)
  between operations  13.6 us (6%)
  other arithmetic  11 us (5%)
    dot_general x2, matrix products, einsum(): return jnp.einsum(form, a.astype(jnp.float32), b.astype(jnp.float32))  91.7 us
    psum x2, waiting for transfers between devices, added(): lax.psum(term.astype(jnp.bfloat16), 'tp').astype(jnp.float32)  72.7 us
    dot_general x1, matrix products, step(): jnp.dot(hidden_of(normed(h, gain_m), w_gate, w_up), w_down, preferred_ele...  17.8 us
    dot_general x1, matrix products, hidden_of(): gate = jnp.dot(b, w_gate, preferred_element_type=jnp.float32)  8.98 us
    dot_general x1, matrix products, step(): h = added(x, jnp.dot(seen, wo, preferred_element_type=jnp.float32))  5.75 us
    dot_general x1, matrix products, matmul(): jnp.dot(a, w, preferred_element_type=jnp.float32).astype(jnp.bfloat16)  5.2 us
  transfers between devices with their start and end apart: 2, of which 2 were waited for; matrix products, arithmetic and copies ran while one was open for 0% of the time, Pallas kernels for 0%

commit v1 on v0

v1 whole, which is shorter than its diff:
```python
import functools

import jax
import jax.numpy as jnp
import numpy as np
from jax import lax
from jax.experimental import pallas as pl
from jax.experimental.pallas import tpu as pltpu
from jax.sharding import PartitionSpec as P

HEAD = 64
THETA = 10000
T = 1024
NB = 6
G = 16
EARLY = 10

F32, BF16 = jnp.float32, jnp.bfloat16
MESH = pl.DeviceIdType.MESH


def dot(a, b):
    return jnp.dot(a, b, preferred_element_type=F32)


def kernel(
    n, x_hbm, k_hbm, v_hbm, ga_hbm, wq_hbm, wo_hbm, gm_hbm, wg_hbm, wu_hbm, wd_hbm, rot_hbm, out_hbm,
    tiles, x_ref, a_ref, h_ref, q_ref, s_ref, attn_ref, gain_ref, rot_ref, terms, acc_ref, hidden_ref, sums, got, y_ref,
    small_sem, wq_sem, k_sem, v_sem, wo_sem, mlp_sem, t_send, t_recv, s_send, s_recv, y_send, y_recv, out_sem,
):
    me = lax.axis_index("tp")
    batch, d = x_hbm.shape
    width = wq_hbm.shape[1]
    ff = wg_hbm.shape[1]
    heads = width // HEAD
    half = T // 2
    nq, no, nk, nc = d // T, d // T, d // T, ff // half
    ngu = nc * nk
    nd = ff * d // (T * T)
    wq_at = 2 * NB + no
    groups = batch // G

    def peer(i):
        return lax.rem(me + i, n)

    def source(i):
        return lax.rem(me + n - i, n)

    small = [
        pltpu.make_async_copy(s, t, small_sem.at[i])
        for i, (s, t) in enumerate([(x_hbm, x_ref), (ga_hbm, gain_ref.at[0]), (gm_hbm, gain_ref.at[1]), (rot_hbm, rot_ref)])
    ]
    wq = [pltpu.make_async_copy(wq_hbm.at[pl.ds(i * T, T)], tiles.at[wq_at + i], wq_sem.at[i]) for i in range(nq)]
    wo = [pltpu.make_async_copy(wo_hbm.at[:, pl.ds(i * T, T)], tiles.at[2 * NB + i], wo_sem.at[i]) for i in range(no)]

    def keys(b):
        p = lax.rem(b, NB)
        return pltpu.make_async_copy(k_hbm.at[b], tiles.at[2 * p], k_sem.at[p])

    def values(b):
        p = lax.rem(b, NB)
        return pltpu.make_async_copy(v_hbm.at[b], tiles.at[2 * p + 1], v_sem.at[p])

    def gate_up(j, at):
        c, k = j // nk, j % nk
        rows, columns = pl.ds(k * T, T), pl.ds(pl.multiple_of(c * half, half), half)
        return [
            pltpu.make_async_copy(w.at[rows, columns], tiles.at[at, :, pl.ds(i * half, half)], mlp_sem.at[j, i])
            for i, w in enumerate((wg_hbm, wu_hbm))
        ]

    def down(j, at):
        copies = []
        for i in range(2):
            t, r = divmod(2 * j + i, nc)
            columns = pl.ds(pl.multiple_of(peer(1 + t) * T, T), T)
            copies.append(
                pltpu.make_async_copy(wd_hbm.at[pl.ds(r * half, half), columns], tiles.at[at, pl.ds(i * half, half)], mlp_sem.at[ngu + j, i])
            )
        return copies

    freed = [s for b in range(batch - NB, batch) for s in (2 * (b % NB), 2 * (b % NB) + 1)]
    place = [wq_at + j for j in range(EARLY)] + freed + [2 * NB + j for j in range(no)]
    place += [wq_at + j for j in range(ngu + nd - len(place))]

    def mlp(j):
        return gate_up(j, place[j]) if j < ngu else down(j - ngu, place[j])

    def start(copies):
        for c in copies:
            c.start()

    def wait(copies):
        for c in copies:
            c.wait()

    start(small)
    start(wq)
    for b in range(NB):
        keys(b).start()
        values(b).start()
    start(wo)

    barrier = pltpu.get_barrier_semaphore()
    for i in range(1, n):
        pl.semaphore_signal(barrier, inc=1, device_id={"tp": peer(i)}, device_id_type=MESH)
    pl.semaphore_wait(barrier, n - 1)

    def normed(rows, wide, gain):
        scale = lax.rsqrt(jnp.mean(wide * wide, -1, keepdims=True) + 1e-6)
        a_ref[rows, :] = (wide * scale * gain_ref[gain].astype(F32)).astype(BF16)

    wait(small)

    @pl.loop(0, batch // G)
    def _(g):
        rows = pl.ds(pl.multiple_of(g * G, G), G)
        normed(rows, x_ref[rows, :].astype(F32), 0)

    q = None
    for i in range(nq):
        wq[i].wait()
        part = dot(a_ref[:, i * T : (i + 1) * T], tiles[wq_at + i])
        q = part if q is None else q + part
    q = q.astype(BF16).astype(F32)
    lane = lax.broadcasted_iota(jnp.int32, q.shape, 1)
    other = jnp.where(lane % HEAD < HEAD // 2, pltpu.roll(q, width - HEAD // 2, 1), pltpu.roll(q, HEAD // 2, 1))
    q_ref[...] = (q * rot_ref[0:1, :] + other * rot_ref[1:2, :]).astype(BF16).astype(F32)

    own = lax.broadcasted_iota(jnp.int32, (heads, width), 1) // HEAD == lax.broadcasted_iota(jnp.int32, (heads, width), 0)

    def scores(b):
        q = jnp.where(own, jnp.broadcast_to(q_ref[pl.ds(b, 1), :], (heads, width)), 0.0).astype(BF16)
        return dot(q, tiles[2 * lax.rem(b, NB)])

    def sends(g):
        return [
            pltpu.make_async_remote_copy(
                terms.at[g, me], terms.at[g, me], t_send.at[g, i - 1], t_recv.at[g, i - 1], device_id={"tp": peer(i)}, device_id_type=MESH
            )
            for i in range(1, n)
        ]

    def receives(g):
        return [
            pltpu.make_async_remote_copy(
                terms.at[g, source(i)], terms.at[g, source(i)], t_send.at[g, i - 1], t_recv.at[g, i - 1], device_id={"tp": peer(i)}, device_id_type=MESH
            )
            for i in range(1, n)
        ]

    def finish(g):
        for c in sends(g):
            c.wait_send()
        for c in receives(g):
            c.wait_recv()
        rows = pl.ds(pl.multiple_of(g * G, G), G)
        total = terms[g, 0].astype(F32)
        for i in range(1, n):
            total = total + terms[g, i].astype(F32)
        h = (x_ref[rows, :].astype(F32) + total).astype(BF16)
        h_ref[rows, :] = h
        normed(rows, h.astype(F32), 1)

    keys(0).wait()
    s_ref[...] = scores(0)

    @pl.loop(0, batch)
    def _(b):
        values(b).wait()

        @pl.when(b + 1 < batch)
        def _():
            keys(b + 1).wait()

        later = scores(jnp.minimum(b + 1, batch - 1))
        s = s_ref[...] * HEAD**-0.5
        e = jnp.exp(s - jnp.max(s, -1, keepdims=True))
        w = (e / jnp.sum(e, -1, keepdims=True)).astype(BF16)
        r = lax.dot_general(w, tiles[2 * lax.rem(b, NB) + 1], (((1,), (1,)), ((), ())), preferred_element_type=F32)
        attn_ref[pl.ds(b, 1), :] = jnp.sum(jnp.where(own, r, 0.0), 0, keepdims=True)
        s_ref[...] = later

        @pl.when(b + NB < batch)
        def _():
            keys(b + NB).start()
            values(b + NB).start()

        @pl.when(b == batch - NB - 1)
        def _():
            for j in range(EARLY):
                start(mlp(j))

        @pl.when(jnp.logical_and(b >= batch - NB, b < batch - NB + (ngu - EARLY) // 2))
        def _():
            for i in range(2):
                start(gate_up(EARLY + 2 * (b - (batch - NB)) + i, 2 * lax.rem(b, NB) + i))

        @pl.when(lax.rem(b, G) == G - 1)
        def _():
            g = b // G

            @pl.when(g == 0)
            def _():
                wait(wo)

            part = attn_ref[pl.ds(pl.multiple_of(g * G, G), G), :].astype(BF16)
            for i in range(no):
                terms[g, me, :, i * T : (i + 1) * T] = dot(part, tiles[2 * NB + i]).astype(BF16)
            start(sends(g))

            @pl.when(g > 0)
            def _():
                finish(g - 1)

    for j in range(ngu, EARLY + 2 * NB + no):
        start(mlp(j))
    finish(groups - 1)

    for c in range(nc):
        for k in range(nk):
            j = c * nk + k
            wait(mlp(j))
            part = dot(a_ref[:, k * T : (k + 1) * T], tiles[place[j]])
            if k == 0:
                acc_ref[...] = part
            else:
                acc_ref[...] += part
            if j + EARLY + 2 * NB + no < ngu + nd:
                start(mlp(j + EARLY + 2 * NB + no))
        gate, up = acc_ref[:, :half], acc_ref[:, half:]
        hidden_ref[:, c * half : (c + 1) * half] = (gate * jax.nn.sigmoid(gate) * up).astype(BF16)

    for t in range(n):
        total = None
        for r in range(nc):
            j, i = divmod(t * nc + r, 2)
            if i == 0 or r == 0 and t == 0:
                wait(down(j, place[ngu + j]))
            part = dot(hidden_ref[:, r * half : (r + 1) * half], tiles[place[ngu + j], i * half : (i + 1) * half])
            total = part if total is None else total + part
        if t < n - 1:
            sums[t] = total.astype(BF16)
            pltpu.make_async_remote_copy(
                sums.at[t], got.at[t], s_send.at[t], s_recv.at[t], device_id={"tp": peer(1 + t)}, device_id_type=MESH
            ).start()
    mine = pl.ds(pl.multiple_of(me * T, T), T)
    for t in range(n - 1):
        copy = pltpu.make_async_remote_copy(
            sums.at[t], got.at[t], s_send.at[t], s_recv.at[t], device_id={"tp": peer(1 + t)}, device_id_type=MESH
        )
        copy.wait()
        total = total + got[t].astype(F32)
    y_ref[...] = (h_ref[:, mine].astype(F32) + total).astype(BF16)
    ys = [
        pltpu.make_async_remote_copy(
            y_ref, out_hbm.at[:, mine], y_send.at[i - 1], y_recv.at[i - 1], device_id={"tp": peer(i)}, device_id_type=MESH
        )
        for i in range(1, n)
    ]
    start(ys)
    here = pltpu.make_async_copy(y_ref, out_hbm.at[:, mine], out_sem)
    here.start()
    here.wait()
    for i in range(1, n):
        ys[i - 1].wait_send()
        theirs = pl.ds(pl.multiple_of(source(i) * T, T), T)
        pltpu.make_async_remote_copy(
            y_ref, out_hbm.at[:, theirs], y_send.at[i - 1], y_recv.at[i - 1], device_id={"tp": peer(i)}, device_id_type=MESH
        ).wait_recv()


def solution(mesh):
    n = mesh.shape["tp"]

    def step(x, k_cache, v_cache, gain_a, wq, wo, gain_m, w_gate, w_up, w_down):
        batch, cache, heads, head = k_cache.shape
        d, width = wq.shape
        ff = w_gate.shape[1]
        k = jnp.transpose(k_cache, (0, 2, 3, 1)).reshape(batch, width, cache)
        v = jnp.transpose(v_cache, (0, 2, 3, 1)).reshape(batch, width, cache)
        angle = np.float32(cache - 1) * np.float32(THETA) ** (-np.arange(head // 2, dtype=np.float32) / np.float32(head // 2))
        cos, sin = np.cos(angle), np.sin(angle)
        rot = np.stack([np.tile(np.concatenate(c), heads) for c in ((cos, cos), (-sin, sin))]).astype(np.float32)
        no, nd, ngu = d // T, ff * d // (T * T), 2 * ff * d // (T * T)
        groups = batch // G
        dma = pltpu.SemaphoreType.DMA
        anywhere = pl.BlockSpec(memory_space=pl.ANY)
        return pl.pallas_call(
            functools.partial(kernel, n),
            out_shape=jax.ShapeDtypeStruct((batch, d), BF16),
            in_specs=[anywhere] * 11,
            out_specs=anywhere,
            scratch_shapes=[
                pltpu.VMEM((2 * NB + no + EARLY, T, T), BF16),
                pltpu.VMEM((batch, d), BF16),
                pltpu.VMEM((batch, d), BF16),
                pltpu.VMEM((batch, d), BF16),
                pltpu.VMEM((batch, width), F32),
                pltpu.VMEM((heads, cache), F32),
                pltpu.VMEM((batch, width), F32),
                pltpu.VMEM((2, 1, d), BF16),
                pltpu.VMEM((2, width), F32),
                pltpu.VMEM((groups, n, G, d), BF16),
                pltpu.VMEM((batch, T), F32),
                pltpu.VMEM((batch, ff), BF16),
                pltpu.VMEM((n - 1, batch, T), BF16),
                pltpu.VMEM((n - 1, batch, T), BF16),
                pltpu.VMEM((batch, T), BF16),
                dma((4,)), dma((d // T,)), dma((NB,)), dma((NB,)), dma((no,)), dma((ngu + nd, 2)),
                dma((groups, n - 1)), dma((groups, n - 1)), dma((n - 1,)), dma((n - 1,)), dma((n - 1,)), dma((n - 1,)), dma,
            ],
            compiler_params=pltpu.CompilerParams(collective_id=0, has_side_effects=True, vmem_limit_bytes=67043328),
            name="layer",
        )(x, k, v, gain_a.reshape(1, d), wq, wo, gain_m.reshape(1, d), w_gate, w_up, w_down, rot)

    states, cache, columns, rows_of = P("dp", None), P("dp", None, "tp", None), P(None, "tp"), P("tp", None)
    return jax.shard_map(
        step,
        mesh=mesh,
        in_specs=(states, cache, cache, P(None), columns, rows_of, P(None), columns, columns, rows_of),
        out_specs=states,
        check_vma=False,
    )
```

time: 229 us -> 131 us (0.57)
  matrix products: 129 us -> 0 us
  Pallas kernels: 0 us -> 126 us
  waiting for transfers between devices: 72.8 us -> 0 us
  between operations: 13.6 us -> 0.01 us
  other arithmetic: 11 us -> 0 us
  local copies, waits for them, and re-layouts: 1.09 us -> 4.48 us
    dot_general x6 -> x0, matrix products: 129 us -> none  [the longest x2 91.7 us: einsum(): return jnp.einsum(form, a.astype(jnp.float32), b.astype(jnp.float32))]
    pallas_call x0 -> x1, Pallas kernels: none -> 126 us  [step(): pl.pallas_call(functools.partial(kernel, n), out_shape=jax.ShapeDtypeStru...]
    psum x2 -> x0, waiting for transfers between devices: 72.7 us -> none  [added(): lax.psum(term.astype(jnp.bfloat16), 'tp').astype(jnp.float32)]
    sub x1 -> x0, other arithmetic: 3.27 us -> none  [seen_by(): weights = jax.nn.softmax(scores, -1).astype(jnp.bfloat16)]
    convert_element_type x4 -> x0, other arithmetic: 2.7 us -> none  [the longest x1 1.96 us: added(): (t.astype(jnp.float32) + lax.psum(term.astype(jnp.bfloat16), 'tp').astype...]
    reduce_sum x2 -> x0, other arithmetic: 2.57 us -> none  [normed(): scale = lax.rsqrt(jnp.mean(wide * wide, -1, keepdims=True) + 1e-06)]
    reshape x1 -> x2, local copies, waits for them, and re-layouts: 0.2 us -> 2.61 us  [the longest x1 1.31 us: step(): gain_a.reshape(1, d)]
  transfers between devices with their start and end apart: 2 -> 0, of which waited for: 2 -> 0; matrix products, arithmetic and copies ran while one was open for 0% -> 0% of each run, Pallas kernels for 0% -> 0%
where the time goes in v1:
time: 131 us
  Pallas kernels  126 us (96%)
  local copies, waits for them, and re-layouts  4.48 us (3%)
    pallas_call x1, Pallas kernels, step(): pl.pallas_call(functools.partial(kernel, n), out_shape=jax.ShapeDtypeStru...  126 us

profile of v1, /device:TPU:112, one launch (start us, length us, event | category | flops | bytes accessed | tf_op | source)
XLA Modules:
  0.0 130.6 jit_solution(17214190292128461871)
XLA Ops:
  0.0 1.3 %reshape.14.ga_hbm = bf16[1,4096]{1,0:T(2,128)(2,1)} reshape(bf16[4096]{0:T(1024)(128)(2,1)} %param.14) | data formatting | bytes 16384 | tf_op jit(solution)/shard_map/reshape | solution.py:315
  1.3 1.3 reshape.15.gm_hbm
  2.6 126.1 %layer.1 = bf16[64,4096]{1,0:T(8,128)(2,1)} custom-call(bf16[64,4096]{1,0:T(8,128)(2,1)} %x_hbm.1, bf16[64,1024,1024]{2,1,0:T(8,128)(2,1)} %bitcast.1.k_hbm, bf16[64,1024,1024]{2,1,0:T(8,128)(2,1)} %bitcast.3.v_hbm, bf16[1,4096]{1,0:T(2,128)(2,1)} %reshape.14.ga_hbm, bf16[4096,1024]{1,0:T(8,128)(2,1)} %wq_hbm.1, bf16[1024,4096]{1,0:T(8,128)(2,1)} %wo_hbm.1, ...), custom_call_target="tpu_custom_call" | custom-call | tf_op jit(solution)/shard_map/layer/pallas_call | solution.py:289
  128.8 1.9 %copy.13 = bf16[64,4096]{1,0:T(8,128)(2,1)} copy(bf16[64,4096]{1,0:T(8,128)(2,1)} %layer.1) | data formatting | bytes 1048576

commit v2 on v1

--- a/solution.py
+++ b/solution.py
@@ -11,9 +11,10 @@
 HEAD = 64
 THETA = 10000
 T = 1024
-NB = 6
-G = 16
-EARLY = 10
+AHEAD = 4
+NB = AHEAD + 1
+G = 8
+EARLY = 12
 
 F32, BF16 = jnp.float32, jnp.bfloat16
 MESH = pl.DeviceIdType.MESH
@@ -23,10 +24,14 @@
     return jnp.dot(a, b, preferred_element_type=F32)
 
 
+def few(a, b):
+    return dot(jnp.concatenate([a, a], 0), b)
+
+
 def kernel(
-    n, x_hbm, k_hbm, v_hbm, ga_hbm, wq_hbm, wo_hbm, gm_hbm, wg_hbm, wu_hbm, wd_hbm, rot_hbm, out_hbm,
-    tiles, x_ref, a_ref, h_ref, q_ref, s_ref, attn_ref, gain_ref, rot_ref, terms, acc_ref, hidden_ref, sums, got, y_ref,
-    small_sem, wq_sem, k_sem, v_sem, wo_sem, mlp_sem, t_send, t_recv, s_send, s_recv, y_send, y_recv, out_sem,
+    n, x_hbm, k_hbm, v_hbm, ga_hbm, wq_hbm, wo_hbm, gm_hbm, wg_hbm, wu_hbm, wd_hbm, rot_hbm, out_ref,
+    tiles, x_ref, a_ref, h_ref, normed_ref, q_ref, s_ref, attn_ref, gain_ref, wide_gain, rot_ref, terms, hidden_ref, sums, passing, waiting, got,
+    small_sem, wq_sem, k_sem, v_sem, wo_sem, mlp_sem, t_send, t_recv, p_send, p_recv, s_send, s_recv, y_send, y_recv,
 ):
     me = lax.axis_index("tp")
     batch, d = x_hbm.shape
@@ -37,6 +42,7 @@
     nq, no, nk, nc = d // T, d // T, d // T, ff // half
     ngu = nc * nk
     nd = ff * d // (T * T)
+    turns = (2, 1, n - 1, 0)
     wq_at = 2 * NB + no
     groups = batch // G
 
@@ -73,7 +79,7 @@
         copies = []
         for i in range(2):
             t, r = divmod(2 * j + i, nc)
-            columns = pl.ds(pl.multiple_of(peer(1 + t) * T, T), T)
+            columns = pl.ds(pl.multiple_of(peer(turns[t]) * T, T), T)
             copies.append(
                 pltpu.make_async_copy(wd_hbm.at[pl.ds(r * half, half), columns], tiles.at[at, pl.ds(i * half, half)], mlp_sem.at[ngu + j, i])
             )
@@ -96,28 +102,34 @@
 
     start(small)
     start(wq)
-    for b in range(NB):
-        keys(b).start()
-        values(b).start()
-    start(wo)
 
     barrier = pltpu.get_barrier_semaphore()
     for i in range(1, n):
         pl.semaphore_signal(barrier, inc=1, device_id={"tp": peer(i)}, device_id_type=MESH)
-    pl.semaphore_wait(barrier, n - 1)
-
-    def normed(rows, wide, gain):
+
+    def normed(wide, gain, to, rows):
         scale = lax.rsqrt(jnp.mean(wide * wide, -1, keepdims=True) + 1e-6)
-        a_ref[rows, :] = (wide * scale * gain_ref[gain].astype(F32)).astype(BF16)
+        for c in range(d // 128):
+            at = slice(c * 128, (c + 1) * 128)
+            to[rows, at] = (wide[:, at] * scale * wide_gain[gain, c : c + 1, :]).astype(to.dtype)
 
     wait(small)
-
-    @pl.loop(0, batch // G)
+    for b in range(2):
+        keys(b).start()
+        values(b).start()
+    wide_gain[...] = gain_ref[...].astype(F32)
+
+    @pl.loop(0, batch // 16)
     def _(g):
-        rows = pl.ds(pl.multiple_of(g * G, G), G)
-        normed(rows, x_ref[rows, :].astype(F32), 0)
+        rows = pl.ds(pl.multiple_of(g * 16, 16), 16)
+        wide = x_ref[rows, :].astype(F32)
+        h_ref[rows, :] = wide
+        normed(wide, 0, a_ref, rows)
 
     q = None
+    for b in range(2, AHEAD):
+        keys(b).start()
+        values(b).start()
     for i in range(nq):
         wq[i].wait()
         part = dot(a_ref[:, i * T : (i + 1) * T], tiles[wq_at + i])
@@ -158,15 +170,36 @@
         total = terms[g, 0].astype(F32)
         for i in range(1, n):
             total = total + terms[g, i].astype(F32)
-        h = (x_ref[rows, :].astype(F32) + total).astype(BF16)
+        h = (h_ref[rows, :] + total).astype(BF16).astype(F32)
         h_ref[rows, :] = h
-        normed(rows, h.astype(F32), 1)
-
+        normed(h, 1, normed_ref, pl.ds(pl.multiple_of(lax.rem(g, 2) * G, G), G))
+
+        @pl.when(lax.rem(g, 2) == 1)
+        def _():
+            a_ref[pl.ds(pl.multiple_of((g - 1) * G, 2 * G), 2 * G), :] = normed_ref[...].astype(BF16)
+
+    pl.semaphore_wait(barrier, n - 1)
     keys(0).wait()
     s_ref[...] = scores(0)
 
     @pl.loop(0, batch)
     def _(b):
+        @pl.when(b + AHEAD < batch)
+        def _():
+            keys(b + AHEAD).start()
+            values(b + AHEAD).start()
+
+        @pl.when(b < no)
+        def _():
+            pltpu.make_async_copy(
+                wo_hbm.at[:, pl.ds(pl.multiple_of(b * T, T), T)], tiles.at[2 * NB + b], wo_sem.at[b]
+            ).start()
+
+        @pl.when(b >= batch - AHEAD)
+        def _():
+            for i in range(2):
+                start(gate_up(2 * (b - (batch - AHEAD)) + i, wq_at + 2 * (b - (batch - AHEAD)) + i))
+
         values(b).wait()
 
         @pl.when(b + 1 < batch)
@@ -181,21 +214,6 @@
         attn_ref[pl.ds(b, 1), :] = jnp.sum(jnp.where(own, r, 0.0), 0, keepdims=True)
         s_ref[...] = later
 
-        @pl.when(b + NB < batch)
-        def _():
-            keys(b + NB).start()
-            values(b + NB).start()
-
-        @pl.when(b == batch - NB - 1)
-        def _():
-            for j in range(EARLY):
-                start(mlp(j))
-
-        @pl.when(jnp.logical_and(b >= batch - NB, b < batch - NB + (ngu - EARLY) // 2))
-        def _():
-            for i in range(2):
-                start(gate_up(EARLY + 2 * (b - (batch - NB)) + i, 2 * lax.rem(b, NB) + i))
-
         @pl.when(lax.rem(b, G) == G - 1)
         def _():
             g = b // G
@@ -213,61 +231,90 @@
             def _():
                 finish(g - 1)
 
-    for j in range(ngu, EARLY + 2 * NB + no):
+    for j in range(2 * AHEAD, EARLY + 2 * NB + no):
         start(mlp(j))
     finish(groups - 1)
 
+    quarter = T // 4
+    held = EARLY + 2 * NB + no
     for c in range(nc):
-        for k in range(nk):
-            j = c * nk + k
+        js = range(c * nk, (c + 1) * nk)
+        for j in js:
             wait(mlp(j))
-            part = dot(a_ref[:, k * T : (k + 1) * T], tiles[place[j]])
-            if k == 0:
-                acc_ref[...] = part
+
+        def product(i):
+            product = sum(few(a_ref[:, k * T : (k + 1) * T], tiles[place[j], :, i * quarter : (i + 1) * quarter]) for k, j in enumerate(js))
+            return product[:batch]
+
+        for i in range(2):
+            gate, up = product(i), product(2 + i)
+            hidden_ref[:, c * half + i * quarter : c * half + (i + 1) * quarter] = (gate * jax.nn.sigmoid(gate) * up).astype(BF16)
+        for j in js:
+            if j + held < ngu + nd:
+                start(mlp(j + held))
+
+    right, left = peer(1), peer(n - 1)
+    ways = (right, left)
+    top, bottom = slice(0, batch // 2), slice(batch // 2, batch)
+    halves = (top, bottom)
+
+    def send(src, dst, send_sem, recv_sem, to):
+        return pltpu.make_async_remote_copy(src, dst, send_sem, recv_sem, device_id={"tp": to}, device_id_type=MESH)
+
+    passed = [send(sums.at[0, halves[w]], passing.at[w], p_send.at[w], p_recv.at[w], ways[w]) for w in range(2)]
+    direct = [send(sums.at[1 + w, halves[1 - w]], got.at[w, halves[1 - w]], s_send.at[w, 0], s_recv.at[w, 0], ways[w]) for w in range(2)]
+    added = [send(sums.at[1 + w, halves[w]], got.at[w, halves[w]], s_send.at[w, 1], s_recv.at[w, 1], ways[w]) for w in range(2)]
+    waited = 0
+    for t in range(n):
+        blocks = [divmod(t * nc + r, 2) for r in range(nc)]
+        while waited <= blocks[-1][0]:
+            wait(down(waited, place[ngu + waited]))
+            waited += 1
+        for c in range(4):
+            at = slice(c * quarter, (c + 1) * quarter)
+            total = sum(
+                few(hidden_ref[:, r * half : (r + 1) * half], tiles[place[ngu + j], i * half : (i + 1) * half, at]) for r, (j, i) in enumerate(blocks)
+            )[:batch]
+            if t == 0:
+                sums[0, :, at] = total.astype(BF16)
+            elif t < n - 1:
+                sums[t, halves[2 - t], at] = total[halves[2 - t]].astype(BF16)
+                waiting[t - 1, :, at] = total[halves[t - 1]]
             else:
-                acc_ref[...] += part
-            if j + EARLY + 2 * NB + no < ngu + nd:
-                start(mlp(j + EARLY + 2 * NB + no))
-        gate, up = acc_ref[:, :half], acc_ref[:, half:]
-        hidden_ref[:, c * half : (c + 1) * half] = (gate * jax.nn.sigmoid(gate) * up).astype(BF16)
-
-    for t in range(n):
-        total = None
-        for r in range(nc):
-            j, i = divmod(t * nc + r, 2)
-            if i == 0 or r == 0 and t == 0:
-                wait(down(j, place[ngu + j]))
-            part = dot(hidden_ref[:, r * half : (r + 1) * half], tiles[place[ngu + j], i * half : (i + 1) * half])
-            total = part if total is None else total + part
-        if t < n - 1:
-            sums[t] = total.astype(BF16)
-            pltpu.make_async_remote_copy(
-                sums.at[t], got.at[t], s_send.at[t], s_recv.at[t], device_id={"tp": peer(1 + t)}, device_id_type=MESH
-            ).start()
+                waiting[0, :, at], waiting[1, :, at] = total[top], total[bottom]
+        if t == 0:
+            start(passed)
+        elif t < n - 1:
+            direct[t - 1].start()
+        if t == n - 2:
+            for w in range(2):
+                passed[w].wait()
+                sums[1 + w, halves[w]] = (waiting[w] + passing[w].astype(F32)).astype(BF16)
+                added[w].start()
     mine = pl.ds(pl.multiple_of(me * T, T), T)
-    for t in range(n - 1):
-        copy = pltpu.make_async_remote_copy(
-            sums.at[t], got.at[t], s_send.at[t], s_recv.at[t], device_id={"tp": peer(1 + t)}, device_id_type=MESH
-        )
-        copy.wait()
-        total = total + got[t].astype(F32)
-    y_ref[...] = (h_ref[:, mine].astype(F32) + total).astype(BF16)
-    ys = [
-        pltpu.make_async_remote_copy(
-            y_ref, out_hbm.at[:, mine], y_send.at[i - 1], y_recv.at[i - 1], device_id={"tp": peer(i)}, device_id_type=MESH
-        )
-        for i in range(1, n)
-    ]
-    start(ys)
-    here = pltpu.make_async_copy(y_ref, out_hbm.at[:, mine], out_sem)
-    here.start()
-    here.wait()
-    for i in range(1, n):
-        ys[i - 1].wait_send()
-        theirs = pl.ds(pl.multiple_of(source(i) * T, T), T)
-        pltpu.make_async_remote_copy(
-            y_ref, out_hbm.at[:, theirs], y_send.at[i - 1], y_recv.at[i - 1], device_id={"tp": peer(i)}, device_id_type=MESH
-        ).wait_recv()
+    wait(direct)
+    wait(added)
+    for w in range(2):
+        total = waiting[w] + got[0, halves[w]].astype(F32) + got[1, halves[w]].astype(F32)
+        out_ref[halves[w], mine] = (h_ref[halves[w], mine] + total).astype(BF16)
+
+    def shared(w, i, c, h):
+        block = out_ref.at[halves[h], pl.ds(pl.multiple_of(c * T, T), T)]
+        return send(block, block, y_send.at[w, i], y_recv.at[w, i], ways[w])
+
+    first = [shared(w, 0, me, w) for w in range(2)]
+    second = [shared(w, 1, me, 1 - w) for w in range(2)]
+    third = [shared(w, 2, ways[1 - w], w) for w in range(2)]
+    start(first)
+    start(second)
+    for w in range(2):
+        shared(w, 0, ways[1 - w], w).wait_recv()
+        third[w].start()
+    for w in range(2):
+        shared(w, 1, ways[1 - w], 1 - w).wait_recv()
+        shared(w, 2, peer(2), w).wait_recv()
+    for copy in first + second + third:
+        copy.wait_send()
 
 
 def solution(mesh):
@@ -288,31 +335,33 @@
         anywhere = pl.BlockSpec(memory_space=pl.ANY)
         return pl.pallas_call(
             functools.partial(kernel, n),
-            out_shape=jax.ShapeDtypeStruct((batch, d), BF16),
+            out_shape=pltpu.VMEM((batch, d), BF16),
             in_specs=[anywhere] * 11,
-            out_specs=anywhere,
+            out_specs=pl.BlockSpec(memory_space=pltpu.VMEM),
             scratch_shapes=[
                 pltpu.VMEM((2 * NB + no + EARLY, T, T), BF16),
                 pltpu.VMEM((batch, d), BF16),
                 pltpu.VMEM((batch, d), BF16),
-                pltpu.VMEM((batch, d), BF16),
+                pltpu.VMEM((batch, d), F32),
+                pltpu.VMEM((2 * G, d), F32),
                 pltpu.VMEM((batch, width), F32),
                 pltpu.VMEM((heads, cache), F32),
                 pltpu.VMEM((batch, width), F32),
-                pltpu.VMEM((2, 1, d), BF16),
+                pltpu.VMEM((2, d // 128, 128), BF16),
+                pltpu.VMEM((2, d // 128, 128), F32),
                 pltpu.VMEM((2, width), F32),
                 pltpu.VMEM((groups, n, G, d), BF16),
-                pltpu.VMEM((batch, T), F32),
                 pltpu.VMEM((batch, ff), BF16),
                 pltpu.VMEM((n - 1, batch, T), BF16),
-                pltpu.VMEM((n - 1, batch, T), BF16),
-                pltpu.VMEM((batch, T), BF16),
+                pltpu.VMEM((2, batch // 2, T), BF16),
+                pltpu.VMEM((2, batch // 2, T), F32),
+                pltpu.VMEM((2, batch, T), BF16),
                 dma((4,)), dma((d // T,)), dma((NB,)), dma((NB,)), dma((no,)), dma((ngu + nd, 2)),
-                dma((groups, n - 1)), dma((groups, n - 1)), dma((n - 1,)), dma((n - 1,)), dma((n - 1,)), dma((n - 1,)), dma,
+                dma((groups, n - 1)), dma((groups, n - 1)), dma((2,)), dma((2,)), dma((2, 2)), dma((2, 2)), dma((2, 3)), dma((2, 3)),
             ],
-            compiler_params=pltpu.CompilerParams(collective_id=0, has_side_effects=True, vmem_limit_bytes=67043328),
+            compiler_params=pltpu.CompilerParams(collective_id=0, has_side_effects=True, vmem_limit_bytes=65011712),
             name="layer",
-        )(x, k, v, gain_a.reshape(1, d), wq, wo, gain_m.reshape(1, d), w_gate, w_up, w_down, rot)
+        )(x, k, v, gain_a.reshape(d // 128, 128), wq, wo, gain_m.reshape(d // 128, 128), w_gate, w_up, w_down, rot)
 
     states, cache, columns, rows_of = P("dp", None), P("dp", None, "tp", None), P(None, "tp"), P("tp", None)
     return jax.shard_map(

time: 131 us -> 119 us (0.908)
  Pallas kernels: 126 us -> 118 us
  local copies, waits for them, and re-layouts: 4.48 us -> 0.8 us
    pallas_call x1, Pallas kernels: 126 us -> 118 us  [step(): pl.pallas_call(functools.partial(kernel, n), out_shape=pltpu.VMEM((batch,...]
    reshape x2 -> x0, local copies, waits for them, and re-layouts: 2.61 us -> none  [the longest x1 1.31 us: step(): gain_a.reshape(1, d)]
where the time goes in v2:
time: 119 us
  Pallas kernels  118 us (99%)
    pallas_call x1, Pallas kernels, step(): pl.pallas_call(functools.partial(kernel, n), out_shape=pltpu.VMEM((batch,...  118 us

profile of v2, /device:TPU:112, one launch (start us, length us, event | category | flops | bytes accessed | tf_op | source)
XLA Modules:
  0.0 118.7 jit_solution(12372470159314021166)
XLA Ops:
  0.0 117.9 %layer.1 = bf16[64,4096]{1,0:T(8,128)(2,1)S(1)} custom-call(bf16[64,4096]{1,0:T(8,128)(2,1)} %x_hbm.1, bf16[64,1024,1024]{2,1,0:T(8,128)(2,1)} %bitcast.1.k_hbm, bf16[64,1024,1024]{2,1,0:T(8,128)(2,1)} %bitcast.3.v_hbm, bf16[32,128]{1,0:T(8,128)(2,1)} %bitcast.8, bf16[4096,1024]{1,0:T(8,128)(2,1)} %wq_hbm.1, bf16[1024,4096]{1,0:T(8,128)(2,1)} %wo_hbm.1, ...), custom_call_target="tpu_custom_call" | custom-call | tf_op jit(solution)/shard_map/layer/pallas_call | solution.py:336
  117.9 0.8 copy.13

commit v3 on v2

--- a/solution.py
+++ b/solution.py
@@ -30,8 +30,8 @@
 
 def kernel(
     n, x_hbm, k_hbm, v_hbm, ga_hbm, wq_hbm, wo_hbm, gm_hbm, wg_hbm, wu_hbm, wd_hbm, rot_hbm, out_ref,
-    tiles, x_ref, a_ref, h_ref, normed_ref, q_ref, s_ref, attn_ref, gain_ref, wide_gain, rot_ref, terms, hidden_ref, sums, passing, waiting, got,
-    small_sem, wq_sem, k_sem, v_sem, wo_sem, mlp_sem, t_send, t_recv, p_send, p_recv, s_send, s_recv, y_send, y_recv,
+    tiles, x_ref, a_ref, h_ref, normed_ref, q_ref, s_ref, attn_ref, gain_ref, wide_gain, rot_ref, terms, hidden_ref, sums, own_sum, got,
+    small_sem, wq_sem, k_sem, v_sem, wo_sem, mlp_sem, t_send, t_recv, s_send, s_recv, y_send, y_recv,
 ):
     me = lax.axis_index("tp")
     batch, d = x_hbm.shape
@@ -43,6 +43,7 @@
     ngu = nc * nk
     nd = ff * d // (T * T)
     turns = (2, 1, n - 1, 0)
+    order = [(0, 0), (1, 0), (0, 1), (0, 2), (0, 3), (1, 1), (1, 2), (1, 3)]
     wq_at = 2 * NB + no
     groups = batch // G
 
@@ -75,22 +76,21 @@
             for i, w in enumerate((wg_hbm, wu_hbm))
         ]
 
-    def down(j, at):
-        copies = []
-        for i in range(2):
-            t, r = divmod(2 * j + i, nc)
-            columns = pl.ds(pl.multiple_of(peer(turns[t]) * T, T), T)
-            copies.append(
-                pltpu.make_async_copy(wd_hbm.at[pl.ds(r * half, half), columns], tiles.at[at, pl.ds(i * half, half)], mlp_sem.at[ngu + j, i])
-            )
-        return copies
+    def block(i):
+        (s, t), r = order[i // nc], i % nc
+        j, at = i // 4, (pl.ds(i % 4 // 2 * half, half), pl.ds(i % 2 * half, half))
+        return j, at, (pl.ds(r * half, half), pl.ds(pl.multiple_of(peer(turns[t]) * T + s * half, half), half))
+
+    def down(i):
+        j, at, source = block(i)
+        return pltpu.make_async_copy(wd_hbm.at[source], tiles.at[(place[ngu + j], *at)], mlp_sem.at[ngu + j, i % 4])
 
     freed = [s for b in range(batch - NB, batch) for s in (2 * (b % NB), 2 * (b % NB) + 1)]
     place = [wq_at + j for j in range(EARLY)] + freed + [2 * NB + j for j in range(no)]
     place += [wq_at + j for j in range(ngu + nd - len(place))]
 
     def mlp(j):
-        return gate_up(j, place[j]) if j < ngu else down(j - ngu, place[j])
+        return gate_up(j, place[j]) if j < ngu else [down(4 * (j - ngu) + i) for i in range(4)]
 
     def start(copies):
         for c in copies:
@@ -253,68 +253,54 @@
             if j + held < ngu + nd:
                 start(mlp(j + held))
 
-    right, left = peer(1), peer(n - 1)
-    ways = (right, left)
-    top, bottom = slice(0, batch // 2), slice(batch // 2, batch)
-    halves = (top, bottom)
-
     def send(src, dst, send_sem, recv_sem, to):
         return pltpu.make_async_remote_copy(src, dst, send_sem, recv_sem, device_id={"tp": to}, device_id_type=MESH)
 
-    passed = [send(sums.at[0, halves[w]], passing.at[w], p_send.at[w], p_recv.at[w], ways[w]) for w in range(2)]
-    direct = [send(sums.at[1 + w, halves[1 - w]], got.at[w, halves[1 - w]], s_send.at[w, 0], s_recv.at[w, 0], ways[w]) for w in range(2)]
-    added = [send(sums.at[1 + w, halves[w]], got.at[w, halves[w]], s_send.at[w, 1], s_recv.at[w, 1], ways[w]) for w in range(2)]
-    waited = 0
-    for t in range(n):
-        blocks = [divmod(t * nc + r, 2) for r in range(nc)]
-        while waited <= blocks[-1][0]:
-            wait(down(waited, place[ngu + waited]))
-            waited += 1
-        for c in range(4):
-            at = slice(c * quarter, (c + 1) * quarter)
-            total = sum(
-                few(hidden_ref[:, r * half : (r + 1) * half], tiles[place[ngu + j], i * half : (i + 1) * half, at]) for r, (j, i) in enumerate(blocks)
-            )[:batch]
-            if t == 0:
-                sums[0, :, at] = total.astype(BF16)
-            elif t < n - 1:
-                sums[t, halves[2 - t], at] = total[halves[2 - t]].astype(BF16)
-                waiting[t - 1, :, at] = total[halves[t - 1]]
+    def term(s, t):
+        return send(sums.at[s, t], got.at[s, t], s_send.at[s, t], s_recv.at[s, t], peer(turns[t]))
+
+    def columns_of(device, s):
+        return pl.ds(pl.multiple_of(device * T + s * half, half), half)
+
+    def shared(s, i, device):
+        part = out_ref.at[:, columns_of(device, s)]
+        return send(part, part, y_send.at[s, i - 1], y_recv.at[s, i - 1], peer(i))
+
+    def mine(s):
+        return [shared(s, i, me) for i in (2, 1, 3)]
+
+    def finished(s):
+        total = own_sum[s]
+        for t in range(n - 1):
+            term(s, t).wait()
+            total = total + got[s, t].astype(F32)
+        out_ref[:, columns_of(me, s)] = (h_ref[:, columns_of(me, s)] + total).astype(BF16)
+        start(mine(s))
+
+    for at, (s, t) in enumerate(order):
+        blocks = range(at * nc, (at + 1) * nc)
+        for i in blocks:
+            down(i).wait()
+        for c in range(2):
+            total = 0.0
+            for r, i in enumerate(blocks):
+                j, (rows, _), _ = block(i)
+                total += few(hidden_ref[:, r * half : (r + 1) * half], tiles[place[ngu + j], rows, pl.ds(i % 2 * half + c * quarter, quarter)])
+            total, to = total[:batch], slice(c * quarter, (c + 1) * quarter)
+            if t < n - 1:
+                sums[s, t, :, to] = total.astype(BF16)
             else:
-                waiting[0, :, at], waiting[1, :, at] = total[top], total[bottom]
-        if t == 0:
-            start(passed)
-        elif t < n - 1:
-            direct[t - 1].start()
-        if t == n - 2:
-            for w in range(2):
-                passed[w].wait()
-                sums[1 + w, halves[w]] = (waiting[w] + passing[w].astype(F32)).astype(BF16)
-                added[w].start()
-    mine = pl.ds(pl.multiple_of(me * T, T), T)
-    wait(direct)
-    wait(added)
-    for w in range(2):
-        total = waiting[w] + got[0, halves[w]].astype(F32) + got[1, halves[w]].astype(F32)
-        out_ref[halves[w], mine] = (h_ref[halves[w], mine] + total).astype(BF16)
-
-    def shared(w, i, c, h):
-        block = out_ref.at[halves[h], pl.ds(pl.multiple_of(c * T, T), T)]
-        return send(block, block, y_send.at[w, i], y_recv.at[w, i], ways[w])
-
-    first = [shared(w, 0, me, w) for w in range(2)]
-    second = [shared(w, 1, me, 1 - w) for w in range(2)]
-    third = [shared(w, 2, ways[1 - w], w) for w in range(2)]
-    start(first)
-    start(second)
-    for w in range(2):
-        shared(w, 0, ways[1 - w], w).wait_recv()
-        third[w].start()
-    for w in range(2):
-        shared(w, 1, ways[1 - w], 1 - w).wait_recv()
-        shared(w, 2, peer(2), w).wait_recv()
-    for copy in first + second + third:
-        copy.wait_send()
+                own_sum[s, :, to] = total
+        if t < n - 1:
+            term(s, t).start()
+        if (s, t) == (1, n - 2):
+            finished(0)
+    finished(1)
+    for s in range(2):
+        for i in range(1, n):
+            shared(s, i, source(i)).wait_recv()
+        for copy in mine(s):
+            copy.wait_send()
 
 
 def solution(mesh):
@@ -352,12 +338,11 @@
                 pltpu.VMEM((2, width), F32),
                 pltpu.VMEM((groups, n, G, d), BF16),
                 pltpu.VMEM((batch, ff), BF16),
-                pltpu.VMEM((n - 1, batch, T), BF16),
-                pltpu.VMEM((2, batch // 2, T), BF16),
-                pltpu.VMEM((2, batch // 2, T), F32),
-                pltpu.VMEM((2, batch, T), BF16),
-                dma((4,)), dma((d // T,)), dma((NB,)), dma((NB,)), dma((no,)), dma((ngu + nd, 2)),
-                dma((groups, n - 1)), dma((groups, n - 1)), dma((2,)), dma((2,)), dma((2, 2)), dma((2, 2)), dma((2, 3)), dma((2, 3)),
+                pltpu.VMEM((2, n - 1, batch, T // 2), BF16),
+                pltpu.VMEM((2, batch, T // 2), F32),
+                pltpu.VMEM((2, n - 1, batch, T // 2), BF16),
+                dma((4,)), dma((d // T,)), dma((NB,)), dma((NB,)), dma((no,)), dma((ngu + nd, 4)),
+                dma((groups, n - 1)), dma((groups, n - 1)), dma((2, n - 1)), dma((2, n - 1)), dma((2, n - 1)), dma((2, n - 1)),
             ],
             compiler_params=pltpu.CompilerParams(collective_id=0, has_side_effects=True, vmem_limit_bytes=65011712),
             name="layer",

time: 119 us -> 117 us (0.983)
  Pallas kernels: 118 us -> 116 us
    pallas_call x1, Pallas kernels: 118 us -> 116 us  [step(): pl.pallas_call(functools.partial(kernel, n), out_shape=pltpu.VMEM((batch,...]
where the time goes in v3:
time: 117 us
  Pallas kernels  116 us (99%)
    pallas_call x1, Pallas kernels, step(): pl.pallas_call(functools.partial(kernel, n), out_shape=pltpu.VMEM((batch,...  116 us

profile of v3, /device:TPU:112, one launch (start us, length us, event | category | flops | bytes accessed | tf_op | source)
XLA Modules:
  0.0 116.6 jit_solution(7142780039149541159)
XLA Ops:
  0.0 115.8 %layer.1 = bf16[64,4096]{1,0:T(8,128)(2,1)S(1)} custom-call(bf16[64,4096]{1,0:T(8,128)(2,1)} %x_hbm.1, bf16[64,1024,1024]{2,1,0:T(8,128)(2,1)} %bitcast.1.k_hbm, bf16[64,1024,1024]{2,1,0:T(8,128)(2,1)} %bitcast.3.v_hbm, bf16[32,128]{1,0:T(8,128)(2,1)} %bitcast.8, bf16[4096,1024]{1,0:T(8,128)(2,1)} %wq_hbm.1, bf16[1024,4096]{1,0:T(8,128)(2,1)} %wo_hbm.1, ...), custom_call_target="tpu_custom_call" | custom-call | tf_op jit(solution)/shard_map/layer/pallas_call | solution.py:322
  115.8 0.8 copy.13
